TPU v7x, 32 devices: a whole 2x2x4 slice. The times are simulated.
32 devices in a mesh: dp: 4 (over x, core), tensor: 8 (over z, y).
Axes of the slice: x: 2, y: 2, z: 4, core: 2. Of those that a mesh axis runs over, the one named last changes fastest.
Arguments:
- out_grad: bfloat16 [2, 320, 4096], P(None, 'dp', 'tensor'), may hold values from -0.3125 to 0.3125
- layer_input: bfloat16 [2, 320, 4096], P(None, 'dp', 'tensor'), may hold values from -8 to 8
- w_down: bfloat16 [16384, 4096], P('tensor'), may hold values from -0.046875 to 0.046875
- silu_gate: bfloat16 [2, 320, 16384], P(None, 'dp', 'tensor'), may hold values from -6 to 6
- up_proj: bfloat16 [2, 320, 16384], P(None, 'dp', 'tensor'), may hold values from -6 to 6
- slope_codes: int32 [2, 32, 16384], P(None, 'dp', 'tensor'), may hold values from 0 to 1073741823
Outputs:
- grad_down: bfloat16 [16384, 4096], P('tensor', 'dp')
- grad_gate: bfloat16 [4096, 16384], P('dp', 'tensor')
- grad_up: bfloat16 [4096, 16384], P('dp', 'tensor')
Inputs may be any that keep to these rules, and one draw needn't show every extreme that they name: `slope_codes`: every word holds ten independent 3-bit codes; all eight codes occur.
All inputs are finite; a program needn't handle non-finite values.
Results may differ from a plain program's by a relative error of at most 0.018.
Values may be sent and summed in bfloat16 or wider, within the bound.
A program may use at most 128 MiB of HBM per device.

v0:
```python
import jax
import jax.numpy as jnp
from jax import lax
from jax.sharding import PartitionSpec as P

SLOPE_LEVELS = (-0.09, 0.06, 0.22, 0.41, 0.6, 0.79, 0.96, 1.08)


def decode_slopes(packed):
    shifts = 3 * jnp.arange(10, dtype=jnp.int32)
    pieces = jnp.bitwise_and(jnp.right_shift(packed[..., None, :], shifts[:, None]), 7)
    pieces = pieces.reshape(packed.shape[:-2] + (packed.shape[-2] * 10, packed.shape[-1]))
    result = jnp.full(pieces.shape, SLOPE_LEVELS[0], jnp.float32)
    for symbol in range(1, 8):
        result = jnp.where(pieces == symbol, jnp.float32(SLOPE_LEVELS[symbol]), result)
    return result


def shards(out_grad, layer_input, w_down, silu_gate, up_proj, slope_codes):
    micro_count = out_grad.shape[0]
    model_width = w_down.shape[1]
    hidden_width = w_down.shape[0]
    group_rows = micro_count * out_grad.shape[1]
    grad_rows, input_rows = (
        lax.all_gather(out_grad, "tensor", axis=2, tiled=True),
        lax.all_gather(layer_input, "tensor", axis=2, tiled=True),
    )
    output_all = grad_rows.reshape(-1, model_width)
    input_all = input_rows.reshape(-1, model_width)
    gate_act = silu_gate.reshape(-1, hidden_width).astype(jnp.float32)
    up_value = up_proj.reshape(-1, hidden_width).astype(jnp.float32)
    hidden = (gate_act * up_value).astype(jnp.bfloat16)
    slopes = decode_slopes(slope_codes).reshape(-1, hidden_width)
    hidden_grad = lax.dot_general(
        output_all, w_down, (((1,), (1,)), ((), ())), preferred_element_type=jnp.float32
    )
    up_grad = (hidden_grad * gate_act).astype(jnp.bfloat16)
    gate_grad = (hidden_grad * up_value * slopes).astype(jnp.bfloat16)
    block_inputs, block_outputs = (
        lax.all_to_all(input_all, "dp", split_axis=1, concat_axis=0, tiled=True),
        lax.all_to_all(output_all, "dp", split_axis=1, concat_axis=0, tiled=True),
    )
    activations = jnp.concatenate((gate_grad, up_grad, hidden), axis=1)
    values = lax.all_gather(activations, "dp", axis=0, tiled=True)
    row_count = values.shape[0]
    groups = row_count // group_rows
    inputs_3d = block_inputs.reshape(groups, group_rows, block_inputs.shape[1])
    outputs_3d = block_outputs.reshape(groups, group_rows, block_outputs.shape[1])
    values_3d = values.reshape(groups, group_rows, values.shape[1])
    gate_up_parts = jnp.einsum(
        "grd,grf->gdf",
        inputs_3d,
        values_3d[:, :, : 2 * hidden_width],
        preferred_element_type=jnp.float32,
    )
    down_parts = jnp.einsum(
        "grf,grd->gfd",
        values_3d[:, :, 2 * hidden_width :],
        outputs_3d,
        preferred_element_type=jnp.float32,
    )
    gate_up_sum = jnp.sum(gate_up_parts.astype(jnp.bfloat16).astype(jnp.float32), axis=0)
    down_sum = jnp.sum(down_parts.astype(jnp.bfloat16).astype(jnp.float32), axis=0)
    grad_down = down_sum.astype(jnp.bfloat16)
    grad_gate = gate_up_sum[:, :hidden_width].astype(jnp.bfloat16)
    grad_up = gate_up_sum[:, hidden_width:].astype(jnp.bfloat16)
    return (grad_down, grad_gate, grad_up)


def solution(mesh):
    return jax.shard_map(
        shards,
        mesh=mesh,
        in_specs=(
            P(None, "dp", "tensor"),
            P(None, "dp", "tensor"),
            P("tensor", None),
            P(None, "dp", "tensor"),
            P(None, "dp", "tensor"),
            P(None, "dp", "tensor"),
        ),
        out_specs=(P("tensor", "dp"), P("dp", "tensor"), P("dp", "tensor")),
        check_vma=False,
    )
```

profile of v0, /device:TPU:0, one launch (start us, length us, event | category | flops | bytes accessed | tf_op | source)
XLA Modules:
  0.0 234.2 jit_solution(13841438188736707465)
XLA Ops:
  7.2 0.0 all-gather.4.cloned.1.call-start
  7.2 0.7 all-gather.4.cloned.1.call-update
  7.9 0.0 all-gather.8.cloned.1.call-start
  7.9 0.7 all-gather.8.cloned.1.call-update
  8.6 0.0 all-gather.6.cloned.1.call-start
  8.7 0.1 shift_right_arithmetic.28
  8.8 0.1 shift_right_arithmetic.30
  8.9 1.1 shift_right_arithmetic.25
  10.0 0.2 shift_right_arithmetic.26
  10.2 44.1 %all-gather.4.cloned.1.call-done = bf16[2,80,4096]{2,1,0:T(8,128)(2,1)} async-done(((bf16[2,80,512]{2,1,0:T(8,128)(2,1)}), bf16[2,80,4096]{2,1,0:T(8,128)(2,1)}) %all-gather.4.cloned.1.call-update) | async-done | bytes 1310736 | tf_op jit(solution)/shard_map/all_gather | solution.py:25
  54.3 12.8 %fusion.4 = (bf16[160,2048]{1,0:T(8,128)(2,1)S(1)}, bf16[160,2048]{1,0:T(8,128)(2,1)S(1)}, bf16[160,2048]{1,0:T(8,128)(2,1)S(1)}) fusion(s32[160,2048]{1,0:T(8,128)S(1)} %shift_right_arithmetic.26, bf16[2,80,2048]{2,1,0:T(8,128)(2,1)} %param.10, s32[160]{0:T(256)S(1)} %shift_right_arithmetic.30, bf16[2,80,2048]{2,1,0:T(8,128)(2,1)} %param.9, ...), kind=kOutput, calls=%fused_computation.10 | convolution fusion | flops 2692546560 | bytes 22676096 | tf_op jit(solution)/shard_map/dot_general | solution.py:34
  67.1 1.4 pad_maximum_fusion
  68.5 0.0 all-gather.6.cloned.1.call-update
  68.5 27.8 %all-gather.8.cloned.1.call-done = bf16[2,80,4096]{2,1,0:T(8,128)(2,1)} async-done(((bf16[2,80,512]{2,1,0:T(8,128)(2,1)}), bf16[2,80,4096]{2,1,0:T(8,128)(2,1)}) %all-gather.8.cloned.1.call-update) | async-done | bytes 1310736 | tf_op jit(solution)/shard_map/all_gather | solution.py:26
  96.3 3.2 %all_to_all.27 = bf16[160,4,1024]{2,1,0:T(4,128)(2,1)S(1)} reshape(bf16[2,80,4096]{2,1,0:T(8,128)(2,1)} %all-gather.8.cloned.1.call-done) | data formatting | bytes 2621440 | tf_op jit(solution)/shard_map/all_to_all | solution.py:40
  99.5 1.4 copy.12
  101.0 0.0 copy-start
  101.0 4.5 %all-to-all-start.1 = ((bf16[160,4,1024]{2,0,1:T(8,128)(2,1)}), bf16[160,4,1024]{2,0,1:T(8,128)(2,1)}, u32[]{:S(2)}, u32[]{:S(2)}) async-start(bf16[160,4,1024]{2,0,1:T(8,128)(2,1)} %copy.12), calls=%async_computation.1 | async-start | bytes 2621440 | tf_op jit(solution)/shard_map/all_to_all | solution.py:40
  105.5 0.0 copy-done
  105.5 1.0 all_to_all.24
  106.5 1.5 copy.11
  108.0 29.0 %all-to-all-done.1 = bf16[160,4,1024]{2,0,1:T(8,128)(2,1)} async-done(((bf16[160,4,1024]{2,0,1:T(8,128)(2,1)}), bf16[160,4,1024]{2,0,1:T(8,128)(2,1)}, u32[]{:S(2)}, u32[]{:S(2)}) %all-to-all-start.1) | async-done | bytes 1310752 | tf_op jit(solution)/shard_map/all_to_all | solution.py:40
  137.0 3.7 %all-to-all-start = ((bf16[160,4,1024]{2,0,1:T(8,128)(2,1)}), bf16[160,4,1024]{2,0,1:T(8,128)(2,1)S(1)}, u32[]{:S(2)}, u32[]{:S(2)}) async-start(bf16[160,4,1024]{2,0,1:T(8,128)(2,1)} %copy.11), calls=%async_computation | async-start | bytes 2621440 | tf_op jit(solution)/shard_map/all_to_all | solution.py:41
  140.8 39.4 %all-gather.6.cloned.1.call-done = bf16[640,6144]{1,0:T(8,128)(2,1)} async-done(((bf16[160,6144]{1,0:T(8,128)(2,1)}), bf16[640,6144]{1,0:T(8,128)(2,1)}) %all-gather.6.cloned.1.call-update) | async-done | bytes 7864336 | tf_op jit(solution)/shard_map/all_gather | solution.py:44
  180.2 19.0 %convert_reduce_fusion = bf16[4096,1024]{1,0:T(8,128)(2,1)} fusion(bf16[4,160,6144]{2,1,0:T(8,128)(2,1)} %bitcast.21, bf16[160,4,1024]{2,0,1:T(8,128)(2,1)} %all-to-all-done.1), kind=kOutput, calls=%fused_computation | convolution fusion | flops 5398069248 | bytes 14942208 | tf_op jit(solution)/shard_map/grd,grf->gdf/dot_general | solution.py:50
  199.2 6.0 %fusion.8 = (bf16[1024,2048]{0,1:T(8,128)(2,1)}, bf16[1024,2048]{0,1:T(8,128)(2,1)}) fusion(bf16[1024,4096]{0,1:T(8,128)(2,1)} %bitcast.19), kind=kLoop, calls=%fused_computation.16 | loop fusion | bytes 16777216 | tf_op jit(solution)/shard_map/slice | solution.py:66
  205.2 6.4 %copy.14 = bf16[1024,2048]{1,0:T(8,128)(2,1)} copy(bf16[1024,2048]{0,1:T(8,128)(2,1)} %get-tuple-element.6) | data formatting | bytes 8388608
  211.6 6.4 %copy.13 = bf16[1024,2048]{1,0:T(8,128)(2,1)} copy(bf16[1024,2048]{0,1:T(8,128)(2,1)} %get-tuple-element.7) | data formatting | bytes 8388608
  218.0 0.0 all-to-all-done
  218.0 9.6 %convert_reduce_fusion.1 = bf16[2048,1024]{1,0:T(8,128)(2,1)} fusion(bf16[4,160,6144]{2,1,0:T(8,128)(2,1)} %bitcast.22, bf16[160,4,1024]{2,0,1:T(8,128)(2,1)S(1)} %all-to-all-done), kind=kOutput, calls=%fused_computation.1 | convolution fusion | flops 2699034624 | bytes 8126464 | tf_op jit(solution)/shard_map/grf,grd->gfd/dot_general | solution.py:56
  (3 shorter events, 0.0 us)
Async XLA Ops:
  7.2 47.2 %all-gather.4.cloned.1.call-start = ((), (), s32[]{:S(2)}) async-start(), calls=%async_computation.2 | async-start | bytes 1474560 | tf_op jit(solution)/shard_map/all_gather | solution.py:25
  7.9 88.4 %all-gather.8.cloned.1.call-start = ((), (), s32[]{:S(2)}) async-start(), calls=%async_computation.4 | async-start | bytes 1474560 | tf_op jit(solution)/shard_map/all_gather | solution.py:26
  8.6 171.5 %all-gather.6.cloned.1.call-start = ((), (), s32[]{:S(2)}) async-start(), calls=%async_computation.3 | async-start | bytes 9830400 | tf_op jit(solution)/shard_map/all_gather | solution.py:44
  101.0 4.5 %copy-start = (bf16[2,80,4096]{2,1,0:T(8,128)(2,1)S(1)}, bf16[2,80,4096]{2,1,0:T(8,128)(2,1)}, u32[]{:S(2)}) copy-start(bf16[2,80,4096]{2,1,0:T(8,128)(2,1)} %all-gather.4.cloned.1.call-done) | copy-start | bytes 3932164
  101.0 36.0 %all-to-all-start.1 = ((bf16[160,4,1024]{2,0,1:T(8,128)(2,1)}), bf16[160,4,1024]{2,0,1:T(8,128)(2,1)}, u32[]{:S(2)}, u32[]{:S(2)}) async-start(bf16[160,4,1024]{2,0,1:T(8,128)(2,1)} %copy.12), calls=%async_computation.1 | async-start | bytes 2621440 | tf_op jit(solution)/shard_map/all_to_all | solution.py:40
  137.0 81.0 %all-to-all-start = ((bf16[160,4,1024]{2,0,1:T(8,128)(2,1)}), bf16[160,4,1024]{2,0,1:T(8,128)(2,1)S(1)}, u32[]{:S(2)}, u32[]{:S(2)}) async-start(bf16[160,4,1024]{2,0,1:T(8,128)(2,1)} %copy.11), calls=%async_computation | async-start | bytes 2621440 | tf_op jit(solution)/shard_map/all_to_all | solution.py:41
Sparse Core Ops, SparseCore 0:
  10.0 44.2 all-gather.3
  56.4 39.8 all-gather.7
  98.4 81.6 all-gather.5
where the time goes:
time: 235 us; the launch traced here: 234 us
  waiting for transfers between devices  142 us (60%)
  matrix products  41.4 us (18%)
  local copies, waits for them, and re-layouts  27.5 us (12%)
  between operations  13.8 us (6%)
  starting transfers between devices  8.34 us (4%)
    all_gather x1, waiting for transfers between devices, shards(): lax.all_gather(out_grad, 'tensor', axis=2, tiled=True)  44.1 us
    all_gather x1, waiting for transfers between devices, shards(): values = lax.all_gather(activations, 'dp', axis=0, tiled=True)  39.4 us
    all_to_all x1, waiting for transfers between devices, shards(): lax.all_to_all(input_all, 'dp', split_axis=1, concat_axis=0, tiled=True)  29 us
    all_gather x1, waiting for transfers between devices, shards(): lax.all_gather(layer_input, 'tensor', axis=2, tiled=True)  27.8 us
    dot_general x1, matrix products, shards(): jnp.einsum('grd,grf->gdf', inputs_3d, values_3d[:, :, :2 * hidden_width],...  19 us
    unnamed x4, local copies, waits for them, and re-layouts  12.8 us
    dot_general x1, matrix products, shards(): lax.dot_general(output_all, w_down, (((1,), (1,)), ((), ())), preferred_e...  12.8 us
    dot_general x1, matrix products, shards(): jnp.einsum('grf,grd->gfd', values_3d[:, :, 2 * hidden_width:], outputs_3d...  9.61 us
  transfers between devices with their start and end apart: 5, of which 4 were waited for; matrix products, arithmetic and copies ran while one was open for 24% of the time, Pallas kernels for 0%

commit v1 on v0

--- a/solution.py
+++ b/solution.py
@@ -4,6 +4,11 @@
 from jax.sharding import PartitionSpec as P
 
 SLOPE_LEVELS = (-0.09, 0.06, 0.22, 0.41, 0.6, 0.79, 0.96, 1.08)
+
+
+def gathered_along(shard, axis, along):
+    parts = lax.all_gather(shard, axis)
+    return jnp.concatenate(parts, axis=along)
 
 
 def decode_slopes(packed):
@@ -22,7 +27,7 @@
     hidden_width = w_down.shape[0]
     group_rows = micro_count * out_grad.shape[1]
     grad_rows, input_rows = (
-        lax.all_gather(out_grad, "tensor", axis=2, tiled=True),
+        gathered_along(out_grad, "tensor", 2),
         lax.all_gather(layer_input, "tensor", axis=2, tiled=True),
     )
     output_all = grad_rows.reshape(-1, model_width)

time: 235 us -> 236 us (level)
  waiting for transfers between devices: 142 us -> 137 us
  local copies, waits for them, and re-layouts: 27.5 us -> 31 us
    all_gather x1, waiting for transfers between devices: 27.8 us -> 22.1 us  [shards(): lax.all_gather(layer_input, 'tensor', axis=2, tiled=True)]
    unnamed x4 -> x3, local copies, waits for them, and re-layouts: 12.8 us -> 14.4 us
  transfers between devices with their start and end apart: 5 -> 5, of which waited for: 4 -> 4; matrix products, arithmetic and copies ran while one was open for 24% -> 27% of each run, Pallas kernels for 0% -> 0%
where the time goes in v1:
time: 236 us; the launch traced here: 235 us
  waiting for transfers between devices  137 us (58%)
  matrix products  42.6 us (18%)
  local copies, waits for them, and re-layouts  31 us (13%)
  between operations  13.8 us (6%)
  starting transfers between devices  8.21 us (3%)
  other arithmetic  2.72 us (1%)
    all_gather x1, waiting for transfers between devices, gathered_along(): parts = lax.all_gather(shard, axis)  44.5 us
    all_gather x1, waiting for transfers between devices, shards(): values = lax.all_gather(activations, 'dp', axis=0, tiled=True)  39.6 us
    all_to_all x1, waiting for transfers between devices, shards(): lax.all_to_all(input_all, 'dp', split_axis=1, concat_axis=0, tiled=True)  29.2 us
    all_gather x1, waiting for transfers between devices, shards(): lax.all_gather(layer_input, 'tensor', axis=2, tiled=True)  22.1 us
    dot_general x1, matrix products, shards(): jnp.einsum('grd,grf->gdf', inputs_3d, values_3d[:, :, :2 * hidden_width],...  19 us
    unnamed x3, local copies, waits for them, and re-layouts  14.4 us
    dot_general x1, matrix products, shards(): lax.dot_general(output_all, w_down, (((1,), (1,)), ((), ())), preferred_e...  14 us
    dot_general x1, matrix products, shards(): jnp.einsum('grf,grd->gfd', values_3d[:, :, 2 * hidden_width:], outputs_3d...  9.62 us
  transfers between devices with their start and end apart: 5, of which 4 were waited for; matrix products, arithmetic and copies ran while one was open for 27% of the time, Pallas kernels for 0%

profile of v1, /device:TPU:0, one launch (start us, length us, event | category | flops | bytes accessed | tf_op | source)
XLA Modules:
  0.0 235.1 jit_solution(9977809601328238962)
XLA Ops:
  7.2 0.0 all-gather.9.cloned.1.call-start
  7.2 0.7 all-gather.9.cloned.1.call-update
  7.9 0.0 all-gather.7.cloned.1.call-start
  7.9 0.7 all-gather.7.cloned.1.call-update
  8.6 0.0 all-gather.5.cloned.1.call-start
  8.7 0.1 shift_right_arithmetic.28
  8.8 0.1 shift_right_arithmetic.30
  8.9 1.1 shift_right_arithmetic.25
  10.0 0.2 shift_right_arithmetic.26
  10.2 44.5 %all-gather.9.cloned.1.call-done = bf16[16,80,512]{2,1,0:T(8,128)(2,1)} async-done(((bf16[2,80,512]{2,1,0:T(8,128)(2,1)}), bf16[16,80,512]{2,1,0:T(8,128)(2,1)}) %all-gather.9.cloned.1.call-update) | async-done | bytes 1310736 | tf_op jit(solution)/shard_map/all_gather | solution.py:10
  54.7 2.0 copy.20
  56.8 1.6 copy.17
  58.3 14.0 %fusion.4 = (bf16[160,2048]{1,0:T(8,128)(2,1)S(1)}, bf16[160,2048]{1,0:T(8,128)(2,1)}, bf16[160,2048]{1,0:T(8,128)(2,1)}) fusion(s32[160,2048]{1,0:T(8,128)S(1)} %shift_right_arithmetic.26, bf16[2,80,2048]{2,1,0:T(8,128)(2,1)} %param.10, s32[160]{0:T(256)S(1)} %shift_right_arithmetic.30, bf16[2,80,2048]{2,1,0:T(8,128)(2,1)} %param.9, ...), kind=kOutput, calls=%fused_computation.10 | convolution fusion | flops 2692546560 | bytes 22676096 | tf_op jit(solution)/shard_map/dot_general | solution.py:39
  72.3 2.7 %pad_maximum_fusion = bf16[160,6144]{1,0:T(8,128)(2,1)} fusion(bf16[160,2048]{1,0:T(8,128)(2,1)} %get-tuple-element.12, bf16[160,2048]{1,0:T(8,128)(2,1)} %get-tuple-element.11, bf16[160,2048]{1,0:T(8,128)(2,1)S(1)} %get-tuple-element.10), kind=kLoop, calls=%fused_computation.4 | loop fusion | flops 5898240 | bytes 3932160 | tf_op jit(solution)/shard_map/concatenate | solution.py:48
  75.0 0.0 all-gather.5.cloned.1.call-update
  75.0 22.1 %all-gather.7.cloned.1.call-done = bf16[2,80,4096]{2,1,0:T(8,128)(2,1)} async-done(((bf16[2,80,512]{2,1,0:T(8,128)(2,1)}), bf16[2,80,4096]{2,1,0:T(8,128)(2,1)}) %all-gather.7.cloned.1.call-update) | async-done | bytes 1310736 | tf_op jit(solution)/shard_map/all_gather | solution.py:31
  97.2 3.2 %all_to_all.27 = bf16[160,4,1024]{2,1,0:T(4,128)(2,1)S(1)} reshape(bf16[2,80,4096]{2,1,0:T(8,128)(2,1)} %all-gather.7.cloned.1.call-done) | data formatting | bytes 2621440 | tf_op jit(solution)/shard_map/all_to_all | solution.py:45
  100.4 1.4 copy.14
  101.9 4.3 %all-to-all-start.1 = ((bf16[160,4,1024]{2,0,1:T(8,128)(2,1)}), bf16[160,4,1024]{2,0,1:T(8,128)(2,1)}, u32[]{:S(2)}, u32[]{:S(2)}) async-start(bf16[160,4,1024]{2,0,1:T(8,128)(2,1)} %copy.14), calls=%async_computation.1 | async-start | bytes 2621440 | tf_op jit(solution)/shard_map/all_to_all | solution.py:45
  106.2 0.9 all_to_all.24
  107.1 1.5 copy.13
  108.6 29.2 %all-to-all-done.1 = bf16[160,4,1024]{2,0,1:T(8,128)(2,1)} async-done(((bf16[160,4,1024]{2,0,1:T(8,128)(2,1)}), bf16[160,4,1024]{2,0,1:T(8,128)(2,1)}, u32[]{:S(2)}, u32[]{:S(2)}) %all-to-all-start.1) | async-done | bytes 1310752 | tf_op jit(solution)/shard_map/all_to_all | solution.py:45
  137.7 3.8 %all-to-all-start = ((bf16[160,4,1024]{2,0,1:T(8,128)(2,1)}), bf16[160,4,1024]{2,0,1:T(8,128)(2,1)S(1)}, u32[]{:S(2)}, u32[]{:S(2)}) async-start(bf16[160,4,1024]{2,0,1:T(8,128)(2,1)} %copy.13), calls=%async_computation | async-start | bytes 2621440 | tf_op jit(solution)/shard_map/all_to_all | solution.py:46
  141.5 39.6 %all-gather.5.cloned.1.call-done = bf16[640,6144]{1,0:T(8,128)(2,1)} async-done(((bf16[160,6144]{1,0:T(8,128)(2,1)}), bf16[640,6144]{1,0:T(8,128)(2,1)}) %all-gather.5.cloned.1.call-update) | async-done | bytes 7864336 | tf_op jit(solution)/shard_map/all_gather | solution.py:49
  181.1 19.0 %convert_reduce_fusion = bf16[4096,1024]{1,0:T(8,128)(2,1)} fusion(bf16[4,160,6144]{2,1,0:T(8,128)(2,1)} %bitcast.32, bf16[160,4,1024]{2,0,1:T(8,128)(2,1)} %all-to-all-done.1), kind=kOutput, calls=%fused_computation | convolution fusion | flops 5398069248 | bytes 14942208 | tf_op jit(solution)/shard_map/grd,grf->gdf/dot_general | solution.py:55
  200.1 6.0 %fusion.8 = (bf16[1024,2048]{0,1:T(8,128)(2,1)}, bf16[1024,2048]{0,1:T(8,128)(2,1)}) fusion(bf16[1024,4096]{0,1:T(8,128)(2,1)} %bitcast.29), kind=kLoop, calls=%fused_computation.17 | loop fusion | bytes 16777216 | tf_op jit(solution)/shard_map/slice | solution.py:71
  206.1 6.4 %copy.16 = bf16[1024,2048]{1,0:T(8,128)(2,1)} copy(bf16[1024,2048]{0,1:T(8,128)(2,1)} %get-tuple-element.6) | data formatting | bytes 8388608
  212.5 6.4 %copy.15 = bf16[1024,2048]{1,0:T(8,128)(2,1)} copy(bf16[1024,2048]{0,1:T(8,128)(2,1)} %get-tuple-element.7) | data formatting | bytes 8388608
  218.9 0.0 all-to-all-done
  219.0 9.6 %convert_reduce_fusion.1 = bf16[2048,1024]{1,0:T(8,128)(2,1)} fusion(bf16[4,160,6144]{2,1,0:T(8,128)(2,1)} %bitcast.33, bf16[160,4,1024]{2,0,1:T(8,128)(2,1)S(1)} %all-to-all-done), kind=kOutput, calls=%fused_computation.1 | convolution fusion | flops 2699034624 | bytes 8126464 | tf_op jit(solution)/shard_map/grf,grd->gfd/dot_general | solution.py:61
  (3 shorter events, 0.0 us)
Async XLA Ops:
  7.2 47.6 %all-gather.9.cloned.1.call-start = ((), (), s32[]{:S(2)}) async-start(), calls=%async_computation.4 | async-start | bytes 1474560 | tf_op jit(solution)/shard_map/all_gather | solution.py:10
  7.9 89.3 %all-gather.7.cloned.1.call-start = ((), (), s32[]{:S(2)}) async-start(), calls=%async_computation.3 | async-start | bytes 1474560 | tf_op jit(solution)/shard_map/all_gather | solution.py:31
  8.6 172.4 %all-gather.5.cloned.1.call-start = ((), (), s32[]{:S(2)}) async-start(), calls=%async_computation.2 | async-start | bytes 9830400 | tf_op jit(solution)/shard_map/all_gather | solution.py:49
  101.9 35.9 %all-to-all-start.1 = ((bf16[160,4,1024]{2,0,1:T(8,128)(2,1)}), bf16[160,4,1024]{2,0,1:T(8,128)(2,1)}, u32[]{:S(2)}, u32[]{:S(2)}) async-start(bf16[160,4,1024]{2,0,1:T(8,128)(2,1)} %copy.14), calls=%async_computation.1 | async-start | bytes 2621440 | tf_op jit(solution)/shard_map/all_to_all | solution.py:45
  137.7 81.2 %all-to-all-start = ((bf16[160,4,1024]{2,0,1:T(8,128)(2,1)}), bf16[160,4,1024]{2,0,1:T(8,128)(2,1)S(1)}, u32[]{:S(2)}, u32[]{:S(2)}) async-start(bf16[160,4,1024]{2,0,1:T(8,128)(2,1)} %copy.13), calls=%async_computation | async-start | bytes 2621440 | tf_op jit(solution)/shard_map/all_to_all | solution.py:46
Sparse Core Ops, SparseCore 0:
  10.2 44.5 all-gather.8
  56.8 40.3 all-gather.6
  99.3 81.6 all-gather.4
